TPU v7x, 32 devices: a whole 2x2x4 slice. The times are simulated.
32 devices in a mesh: gx: 16 (over z, x, core), gy: 2 (over y).
Axes of the slice: x: 2, y: 2, z: 4, core: 2. Of those that a mesh axis runs over, the one named last changes fastest.
Arguments:
- volt: float32 [128, 128, 2048], P('gx', 'gy'), may hold values from -6 to 6
- drive: float32 [128, 128, 2048], P('gx', 'gy'), may hold values from -6 to 6
- region: int32 [128, 128, 32], P('gx', 'gy'), may hold values from 0 to 7
- diode_mask: int32 [128, 128, 32], P('gx', 'gy'), may hold values 0 or 1
- sigma_table: float32 [8], replicated, may hold values from 0.3 to 3
- cap_table: float32 [8], replicated, may hold values from 0.1 to 1
Outputs:
- residual: float32 [128, 128, 2048], P('gx', 'gy')
- coef_norms: float32 [64], replicated
All inputs are finite; a program needn't handle non-finite values. No bound on the sum of `diode_mask` on one device may be relied on, other than what follows from the above.
Results may differ from a plain program's by a relative error of at most 0.0003.
Values sent between devices are 32-bit elements; how exact they have to be, the bound alone decides.
A program may use at most 192 MiB of HBM per device.

v0:
```python
import functools
import math

import jax
import jax.numpy as jnp
import numpy as np
from jax import lax
from jax.experimental import pallas as pl
from jax.experimental.pallas import tpu as pltpu
from jax.sharding import PartitionSpec as P

NZ = 32
H = 32
KC = 64
S = 256
LANES = 128
TILES = NZ * KC // LANES
CHUNK = 8

base_freq = 0.1
norm_eps = 1e-06


def tables():
    orders = np.arange(1, H + 1, dtype=np.float64)
    angles = orders[:, None] * (2.0 * math.pi * np.arange(S) / S)[None, :]
    synthesis = np.concatenate([np.cos(angles), np.sin(angles)], axis=0)
    analysis = synthesis.T * (2.0 / S)
    derived = np.concatenate(
        [base_freq * orders * analysis[:, H:], -base_freq * orders * analysis[:, :H]], axis=1
    )

    def split(table):
        high = table.astype(jnp.bfloat16)
        low = (table - high.astype(np.float64)).astype(jnp.bfloat16)
        return high, low

    high, low = split(synthesis)
    forward = np.concatenate([high, high, low, low], axis=0)
    cell = 0.5 * np.concatenate([analysis, derived], axis=0)
    both = np.zeros((4 * S, LANES))
    both[: 2 * S, :KC] = cell
    both[2 * S :, KC:] = cell
    high, low = split(both)
    return jnp.asarray(forward), jnp.asarray(np.concatenate([high, low], axis=1))


def lookup(region, table, count):
    value = jnp.where(region == 0, table[0], 0.0)
    for r in range(1, count):
        value = jnp.where(region == r, table[r], value)
    return value


def harmonic_mean(left, right):
    return 2.0 * left * right / (left + right)


def spread(cells, tile, lane):
    index = 2 * tile + (lane >= KC).astype(jnp.int32)
    return jnp.take_along_axis(cells, index, axis=1, mode="promise_in_bounds")


def main_kernel(
    rows, cols, regions,
    volt_hbm, ends_hbm, drive_ref, region_ref, mask_ref, end_regions,
    side_ref, side_regions, sigma_ref, cap_ref, forward_ref, back_ref,
    out_ref, squares_ref, volt_buf, cond_buf, cell_buf, side_buf, acc_ref, sems,
):
    i = pl.program_id(0)
    sources = [ends_hbm.at[0]] + [volt_hbm.at[row] for row in range(rows)] + [ends_hbm.at[1]]

    def copy(slot):
        return pltpu.make_async_copy(sources[slot], volt_buf.at[slot], sems.at[slot])

    @pl.when(i == 0)
    def _():
        for slot in range(rows + 2):
            copy(slot).start()
        acc_ref[...] = jnp.zeros_like(acc_ref)
        cond_buf[1 : rows + 1, :, :NZ] = lookup(region_ref[...], sigma_ref, regions)
        cond_buf[0, :, :NZ] = lookup(end_regions[0], sigma_ref, regions)
        cond_buf[rows + 1, :, :NZ] = lookup(end_regions[1], sigma_ref, regions)
        copy(0).wait()
        copy(1).wait()

    for slot in range(2, rows + 2):

        @pl.when(i == slot - 2)
        def _():
            copy(slot).wait()

    lane = lax.broadcasted_iota(jnp.int32, (cols, LANES), 1)
    col = lax.broadcasted_iota(jnp.int32, (cols, LANES), 0)
    cell_buf[0, :, :NZ] = lookup(region_ref[i], cap_ref, regions)
    cell_buf[1, :, :NZ] = mask_ref[i].astype(jnp.float32)
    side_buf[0, :1, :NZ] = lookup(side_regions[0, 0], sigma_ref, regions)
    side_buf[1, :1, :NZ] = lookup(side_regions[1, 0], sigma_ref, regions)
    capacity, diode = cell_buf[0], cell_buf[1]
    cells = cond_buf[i + 1]
    me, count = lax.axis_index("gy"), lax.axis_size("gy")
    has_left, has_right = me > 0, me < count - 1
    g_low = harmonic_mean(cells, cond_buf[i])
    g_high = harmonic_mean(cells, cond_buf[i + 2])
    edge_left = jnp.where(has_left, side_buf[0, :1], 0.0)
    edge_right = jnp.where(has_right, side_buf[1, :1], 0.0)
    cells_after = jnp.where(
        col == cols - 1, jnp.broadcast_to(edge_right, cells.shape), pltpu.roll(cells, cols - 1, 0)
    )
    g_col = harmonic_mean(cells, cells_after)
    g_left = harmonic_mean(cells[:8], jnp.broadcast_to(edge_left, (8, LANES)))
    g_depth = jnp.where(
        lane < NZ - 1, harmonic_mean(cells, pltpu.roll(cells, LANES - 1, 1)), 0.0
    )

    first = lane < KC
    half = lane % KC
    order = base_freq * (half % H + 1).astype(jnp.float32)
    order = jnp.where(half < H, order, -order)
    swap = lane ^ H

    prev_flux = None
    total = jnp.zeros((8, LANES), jnp.float32)
    for start in range(0, TILES, CHUNK):
        xa, xb, turned = [], [], []
        for t in range(start, start + CHUNK):
            v = volt_buf[i + 1, :, t * LANES : (t + 1) * LANES]
            high = v.astype(jnp.bfloat16).astype(jnp.float32)
            low = v - high
            high_r = pltpu.roll(high, KC, 1)
            low_r = pltpu.roll(low, KC, 1)
            xa.append(jnp.where(first, high, low_r).astype(jnp.bfloat16))
            xb.append(jnp.where(first, high_r, low).astype(jnp.bfloat16))
            turned.append(high_r + low_r)
        if start + CHUNK < TILES:
            t = start + CHUNK
            turned.append(pltpu.roll(volt_buf[i + 1, :, t * LANES : (t + 1) * LANES], KC, 1))
        else:
            turned.append(turned[-1])
        x = jnp.concatenate(xa + xb, axis=0)
        samples = jnp.dot(
            jnp.concatenate([x, x], axis=1), forward_ref[...], preferred_element_type=jnp.float32
        )
        size = jnp.abs(samples)
        small = jnp.exp2(size * (-2.0 / math.log(2.0)) - 1.0)
        even = (size + jnp.log(0.5 + small)).astype(jnp.bfloat16)
        charge = jnp.tanh(samples.astype(jnp.bfloat16))
        m = CHUNK * cols
        waves = jnp.concatenate([even[:m], charge[:m], even[m:], charge[m:]], axis=1)
        projected = jnp.dot(waves, back_ref[...], preferred_element_type=jnp.float32)
        projected = projected[:, :LANES] + projected[:, LANES:]
        for t in range(start, start + CHUNK):
            at = slice(t * LANES, (t + 1) * LANES)
            v = volt_buf[i + 1, :, at]
            value = spread(g_low, t, lane) * (v - volt_buf[i, :, at])
            value -= spread(g_high, t, lane) * (volt_buf[i + 2, :, at] - v)
            right = jnp.where(has_right, side_ref[1, 0, :, at], 0.0)
            v_after = jnp.where(
                col == cols - 1, jnp.broadcast_to(right, v.shape), pltpu.roll(v, cols - 1, 0)
            )
            col_flux = spread(g_col, t, lane) * (v_after - v)
            left = jnp.where(has_left, side_ref[0, 0, :, at], 0.0)
            left_flux = spread(g_left, t, lane[:8]) * (v[:8] - jnp.broadcast_to(left, (8, LANES)))
            left_flux = jnp.concatenate([left_flux] * (cols // 8), axis=0)
            value += jnp.where(col == 0, left_flux, pltpu.roll(col_flux, 1, 0)) - col_flux
            v_deep = jnp.where(first, turned[t - start], turned[t - start + 1])
            deep_flux = spread(g_depth, t, lane) * (v_deep - v)
            deep_r = pltpu.roll(deep_flux, KC, 1)
            before = jnp.zeros_like(deep_r) if prev_flux is None else prev_flux
            value += jnp.where(first, before, deep_r) - deep_flux
            prev_flux = deep_r
            swapped = jnp.take_along_axis(v, swap, axis=1, mode="promise_in_bounds")
            value += spread(capacity, t, lane) * (order * swapped)
            rows_of = slice((t - start) * cols, (t - start + 1) * cols)
            value += spread(diode, t, lane) * (projected[rows_of] + 0.5 * v)
            value -= drive_ref[0, :, at]
            out_ref[0, :, at] = value
            total += jnp.sum((value * value).reshape(cols // 8, 8, LANES), axis=0)
    acc_ref[...] += total

    @pl.when(i == rows - 1)
    def _():
        squares_ref[...] = acc_ref[...]


def exchange(axis, count, here, got_ref, send, recv):
    def copy(peer, slot):
        return pltpu.make_async_remote_copy(
            src_ref=got_ref.at[here],
            dst_ref=got_ref.at[slot],
            send_sem=send.at[peer],
            recv_sem=recv.at[slot],
            device_id={axis: peer},
            device_id_type=pl.DeviceIdType.MESH,
        )

    peers = [lax.rem(here + d, count) for d in range(1, count)]
    for peer in peers:
        copy(peer, here).start()
    for peer in peers:
        copy(peer, peer).wait_recv()
    for peer in peers:
        copy(peer, here).wait_send()


def greet(axis, count, here):
    barrier = pltpu.get_barrier_semaphore()
    for d in range(1, count):
        pl.semaphore_signal(
            barrier,
            inc=1,
            device_id={axis: lax.rem(here + d, count)},
            device_id_type=pl.DeviceIdType.MESH,
        )


def norm_of(total, cells):
    value = jnp.broadcast_to(total, (8, LANES))
    value = value + pltpu.roll(value, KC, 1)
    return jnp.sqrt(value / cells + norm_eps)


def reduce_kernel(nx, ny, cells, in_ref, out_ref, got_x, got_y, send_x, recv_x, send_y, recv_y):
    me_x, me_y = lax.axis_index("gx"), lax.axis_index("gy")
    greet("gx", nx, me_x)
    greet("gy", ny, me_y)
    got_x[me_x] = jnp.sum(in_ref[...], axis=0, keepdims=True)
    pl.semaphore_wait(pltpu.get_barrier_semaphore(), nx + ny - 2)
    exchange("gx", nx, me_x, got_x, send_x, recv_x)
    got_y[me_y] = jnp.sum(got_x[...], axis=0)
    exchange("gy", ny, me_y, got_y, send_y, recv_y)
    out_ref[...] = norm_of(jnp.sum(got_y[...], axis=0), cells)


def halo_kernel(
    nx, ny, rows, cols, volt, region, ends, end_regions, sides, side_regions, send, recv,
):
    me_x, me_y = lax.axis_index("gx"), lax.axis_index("gy")
    up, down = lax.rem(me_x + 1, nx), lax.rem(me_x + nx - 1, nx)
    barrier = pltpu.get_barrier_semaphore()
    mesh_ids = pl.DeviceIdType.MESH

    def copy(k, source, target, axis, peer):
        return pltpu.make_async_remote_copy(
            src_ref=source, dst_ref=target, send_sem=send.at[k], recv_sem=recv.at[k],
            device_id={axis: peer}, device_id_type=mesh_ids,
        )

    first, final = pl.ds(0, 1), pl.ds(cols - 1, 1)
    row_copies = [
        copy(0, volt.at[rows - 1], ends.at[0], "gx", up),
        copy(1, volt.at[0], ends.at[1], "gx", down),
        copy(2, region.at[rows - 1], end_regions.at[0], "gx", up),
        copy(3, region.at[0], end_regions.at[1], "gx", down),
    ]
    to_right = [
        copy(4, volt.at[:, final, :], sides.at[0], "gy", me_y + 1),
        copy(5, region.at[:, final, :], side_regions.at[0], "gy", me_y + 1),
    ]
    to_left = [
        copy(6, volt.at[:, first, :], sides.at[1], "gy", me_y - 1),
        copy(7, region.at[:, first, :], side_regions.at[1], "gy", me_y - 1),
    ]
    has_left, has_right = me_y > 0, me_y < ny - 1

    pl.semaphore_signal(barrier, inc=1, device_id={"gx": up}, device_id_type=mesh_ids)
    pl.semaphore_signal(barrier, inc=1, device_id={"gx": down}, device_id_type=mesh_ids)

    @pl.when(has_right)
    def _():
        pl.semaphore_signal(barrier, inc=1, device_id={"gy": me_y + 1}, device_id_type=mesh_ids)

    @pl.when(has_left)
    def _():
        pl.semaphore_signal(barrier, inc=1, device_id={"gy": me_y - 1}, device_id_type=mesh_ids)

    greeted = 2 + jnp.where(has_right, 1, 0) + jnp.where(has_left, 1, 0)
    pl.semaphore_wait(barrier, greeted)

    for c in row_copies:
        c.start()

    @pl.when(has_right)
    def _():
        for c in to_right:
            c.start()

    @pl.when(has_left)
    def _():
        for c in to_left:
            c.start()

    for c in row_copies:
        c.wait_recv()
        c.wait_send()

    @pl.when(has_right)
    def _():
        for c in to_right:
            c.wait_send()
        for c in to_left:
            c.wait_recv()

    @pl.when(has_left)
    def _():
        for c in to_left:
            c.wait_send()
        for c in to_right:
            c.wait_recv()


def body(volt, drive, region, diode_mask, sigma_table, cap_table):
    rows, cols, width = volt.shape
    regions = sigma_table.shape[0]
    nx, ny = lax.axis_size("gx"), lax.axis_size("gy")
    anywhere = pl.BlockSpec(memory_space=pl.ANY)
    shaped = lambda *shape: jax.ShapeDtypeStruct(shape, jnp.float32)
    ends, end_regions, sides, side_regions = pl.pallas_call(
        functools.partial(halo_kernel, nx, ny, rows, cols),
        out_shape=(
            shaped(2, cols, width),
            jax.ShapeDtypeStruct((2, cols, NZ), jnp.int32),
            shaped(2, rows, 1, width),
            jax.ShapeDtypeStruct((2, rows, 1, NZ), jnp.int32),
        ),
        in_specs=[anywhere] * 2,
        out_specs=(anywhere,) * 4,
        scratch_shapes=[pltpu.SemaphoreType.DMA((8,)), pltpu.SemaphoreType.DMA((8,))],
        compiler_params=pltpu.CompilerParams(collective_id=1, has_side_effects=True),
        name="halos",
    )(volt, region)
    forward, back = tables()

    whole = lambda *shape: pl.BlockSpec(shape, lambda i: (0,) * len(shape))
    row_spec = pl.BlockSpec((1, cols, width), lambda i: (i, 0, 0))
    side_map = lambda i: (0, i, 0, 0)
    smem = pl.BlockSpec(memory_space=pltpu.SMEM)
    residual, sums = pl.pallas_call(
        functools.partial(main_kernel, rows, cols, regions),
        grid=(rows,),
        out_shape=(shaped(*volt.shape), shaped(8, LANES)),
        in_specs=[
            anywhere,
            anywhere,
            row_spec,
            whole(rows, cols, NZ),
            whole(rows, cols, NZ),
            whole(2, cols, NZ),
            pl.BlockSpec((2, 1, 1, width), side_map),
            pl.BlockSpec((2, 1, 1, NZ), side_map),
            smem,
            smem,
            whole(*forward.shape),
            whole(*back.shape),
        ],
        out_specs=(row_spec, whole(8, LANES)),
        scratch_shapes=[
            pltpu.VMEM((rows + 2, cols, width), jnp.float32),
            pltpu.VMEM((rows + 2, cols, LANES), jnp.float32),
            pltpu.VMEM((2, cols, LANES), jnp.float32),
            pltpu.VMEM((2, 8, LANES), jnp.float32),
            pltpu.VMEM((8, LANES), jnp.float32),
            pltpu.SemaphoreType.DMA((rows + 2,)),
        ],
        compiler_params=pltpu.CompilerParams(
            dimension_semantics=("arbitrary",), vmem_limit_bytes=50 * 2**20
        ),
        name="cells",
    )(
        volt, ends, drive, region, diode_mask, end_regions, sides, side_regions,
        sigma_table, cap_table, forward, back,
    )

    norms = pl.pallas_call(
        functools.partial(reduce_kernel, nx, ny, float(rows * cols * NZ * nx * ny)),
        out_shape=jax.ShapeDtypeStruct((8, LANES), jnp.float32),
        in_specs=[pl.BlockSpec(memory_space=pltpu.VMEM)],
        out_specs=pl.BlockSpec(memory_space=pltpu.VMEM),
        scratch_shapes=[
            pltpu.VMEM((nx, 1, LANES), jnp.float32),
            pltpu.VMEM((ny, 1, LANES), jnp.float32),
            pltpu.SemaphoreType.DMA((nx,)),
            pltpu.SemaphoreType.DMA((nx,)),
            pltpu.SemaphoreType.DMA((ny,)),
            pltpu.SemaphoreType.DMA((ny,)),
        ],
        compiler_params=pltpu.CompilerParams(collective_id=0, has_side_effects=True),
        name="norms",
    )(sums)
    return residual, norms[0, :KC]


def solution(mesh):
    return jax.shard_map(
        body,
        mesh=mesh,
        in_specs=(
            P("gx", "gy", None),
            P("gx", "gy", None),
            P("gx", "gy", None),
            P("gx", "gy", None),
            P(),
            P(),
        ),
        out_specs=(P("gx", "gy", None), P()),
        check_vma=False,
    )
```

profile of v0, /device:TPU:0, one launch (start us, length us, event | category | flops | bytes accessed | tf_op | source)
XLA Modules:
  0.0 65.0 jit_solution(8359191785003581124)
XLA Ops:
  0.6 0.0 copy-start.2
  0.6 0.0 copy-start.3
  0.7 0.0 copy-start.9
  0.7 0.0 copy-start.8
  0.7 1.8 %copy.10.region.region_ref = s32[8,64,32]{2,1,0:T(8,128)} copy(s32[8,64,32]{1,2,0:T(8,128)} %param.10) | data formatting | bytes 131072 | tf_op args[2]
  2.5 0.0 copy-start
  2.5 1.1 %copy.12.mask_ref = s32[8,64,32]{2,1,0:T(8,128)S(1)} copy(s32[8,64,32]{1,2,0:T(8,128)} %param.11) | data formatting | bytes 131072 | tf_op args[3]
  3.6 14.5 %halos.1 = (f32[2,64,2048]{2,1,0:T(8,128)}, s32[2,64,32]{2,1,0:T(8,128)}, f32[2,8,1,2048]{3,2,1,0:T(1,128)}, s32[2,8,1,32]{3,2,1,0:T(1,128)}) custom-call(f32[8,64,2048]{2,1,0:T(8,128)} %volt_hbm.1, s32[8,64,32]{2,1,0:T(8,128)} %copy.10.region.region_ref), custom_call_target="tpu_custom_call" | custom-call | tf_op jit(solution)/shard_map/halos/pallas_call | solution.py:318
  18.1 0.0 copy-done.2
  18.1 0.0 copy-done.3
  18.1 0.0 copy-done.9
  18.1 0.0 copy-done.8
  18.1 0.0 copy-done
  18.1 0.0 copy-start.1
  18.2 1.2 %copy-done.1 = f32[2,64,2048]{2,1,0:T(8,128)S(1)} copy-done((f32[2,64,2048]{2,1,0:T(8,128)S(1)}, f32[2,64,2048]{2,1,0:T(8,128)}, u32[]{:S(2)}) %copy-start.1) | copy-done | bytes 1048600
  19.4 0.0 copy-start.4
  19.4 0.9 %copy-done.4 = f32[2,8,1,2048]{3,2,1,0:T(1,128)S(1)} copy-done((f32[2,8,1,2048]{3,2,1,0:T(1,128)S(1)}, f32[2,8,1,2048]{3,2,1,0:T(1,128)}, u32[]{:S(2)}) %copy-start.4) | copy-done | bytes 131096
  20.3 0.0 copy-start.5
  20.3 0.8 %copy-done.5 = s32[2,64,32]{2,1,0:T(8,128)S(1)} copy-done((s32[2,64,32]{2,1,0:T(8,128)S(1)}, s32[2,64,32]{2,1,0:T(8,128)}, u32[]{:S(2)}) %copy-start.5) | copy-done | bytes 16408
  21.1 0.0 copy-start.6
  21.1 0.7 %copy-done.6 = s32[2,8,1,32]{3,2,1,0:T(1,128)S(1)} copy-done((s32[2,8,1,32]{3,2,1,0:T(1,128)S(1)}, s32[2,8,1,32]{3,2,1,0:T(1,128)}, u32[]{:S(2)}) %copy-start.6) | copy-done | bytes 2072
  21.8 27.6 %cells.1 = (f32[8,64,2048]{2,1,0:T(8,128)}, f32[8,128]{1,0:T(8,128)S(1)}) custom-call(f32[8,64,2048]{2,1,0:T(8,128)} %volt_hbm.1, f32[2,64,2048]{2,1,0:T(8,128)S(1)} %copy-done.1, f32[8,64,2048]{2,1,0:T(8,128)} %drive_ref.1, s32[8,64,32]{2,1,0:T(8,128)S(1)} %copy-done, s32[8,64,32]{2,1,0:T(8,128)S(1)} %copy.12.mask_ref, s32[2,64,32]{2,1,0:T(8,128)S(1)} %copy-done.5, ...), custom_call_target="tpu_custom_call" | custom-call | tf_op jit(solution)/shard_map/cells/pallas_call | solution.py:338
  49.4 0.0 copy-start.7
  49.4 0.6 copy-done.7
  50.0 13.9 %norms.1 = f32[8,128]{1,0:T(8,128)} custom-call(f32[8,128]{1,0:T(8,128)} %copy-done.7), custom_call_target="tpu_custom_call" | custom-call | tf_op jit(solution)/shard_map/norms/pallas_call | solution.py:374
  63.8 1.2 %slice_bitcast_fusion = f32[64]{0:T(128)} fusion(f32[8,128]{1,0:T(8,128)} %norms.1), kind=kLoop, calls=%fused_computation | loop fusion | bytes 512 | tf_op jit(solution)/shard_map/squeeze | solution.py:390
Async XLA Ops:
  0.6 17.5 %copy-start.2 = (bf16[1024,256]{1,0:T(8,128)(2,1)S(1)}, bf16[1024,256]{1,0:T(8,128)(2,1)}, u32[]{:S(2)}) copy-start(bf16[1024,256]{1,0:T(8,128)(2,1)} %constant.5.clone.back_ref) | copy-start | bytes 1572868
  0.6 17.5 %copy-start.3 = (bf16[256,256]{1,0:T(8,128)(2,1)S(1)}, bf16[256,256]{1,0:T(8,128)(2,1)}, u32[]{:S(2)}) copy-start(bf16[256,256]{1,0:T(8,128)(2,1)} %constant.4.clone.forward_ref) | copy-start | bytes 393220
  0.7 17.5 %copy-start.9 = (f32[8]{0:T(128)S(1)}, f32[8]{0:T(128)}, u32[]{:S(2)}) copy-start(f32[8]{0:T(128)} %cap_ref.1) | copy-start | bytes 100
  0.7 17.5 %copy-start.8 = (f32[8]{0:T(128)S(1)}, f32[8]{0:T(128)}, u32[]{:S(2)}) copy-start(f32[8]{0:T(128)} %sigma_ref.1) | copy-start | bytes 100
  2.5 15.7 %copy-start = (s32[8,64,32]{2,1,0:T(8,128)S(1)}, s32[8,64,32]{2,1,0:T(8,128)}, u32[]{:S(2)}) copy-start(s32[8,64,32]{2,1,0:T(8,128)} %copy.10.region.region_ref) | copy-start | bytes 196612
  18.1 1.2 %copy-start.1 = (f32[2,64,2048]{2,1,0:T(8,128)S(1)}, f32[2,64,2048]{2,1,0:T(8,128)}, u32[]{:S(2)}) copy-start(f32[2,64,2048]{2,1,0:T(8,128)} %get-tuple-element.8.ends_hbm) | copy-start | bytes 3145732
  19.4 0.9 %copy-start.4 = (f32[2,8,1,2048]{3,2,1,0:T(1,128)S(1)}, f32[2,8,1,2048]{3,2,1,0:T(1,128)}, u32[]{:S(2)}) copy-start(f32[2,8,1,2048]{3,2,1,0:T(1,128)} %get-tuple-element.10.side_ref) | copy-start | bytes 393220
  20.3 0.8 %copy-start.5 = (s32[2,64,32]{2,1,0:T(8,128)S(1)}, s32[2,64,32]{2,1,0:T(8,128)}, u32[]{:S(2)}) copy-start(s32[2,64,32]{2,1,0:T(8,128)} %get-tuple-element.9.end_regions) | copy-start | bytes 49156
  21.1 0.7 %copy-start.6 = (s32[2,8,1,32]{3,2,1,0:T(1,128)S(1)}, s32[2,8,1,32]{3,2,1,0:T(1,128)}, u32[]{:S(2)}) copy-start(s32[2,8,1,32]{3,2,1,0:T(1,128)} %get-tuple-element.11.side_regions) | copy-start | bytes 6148
  49.4 0.6 copy-start.7
where the time goes:
time: 65.4 us; the launch traced here: 65 us
  Pallas kernels  56 us (86%)
  local copies, waits for them, and re-layouts  8.32 us (13%)
  between operations  0.75 us (1%)
    pallas_call x1, Pallas kernels, body(): pl.pallas_call(functools.partial(main_kernel, rows, cols, regions), grid=...  27.6 us
    pallas_call x1, Pallas kernels, body(): pl.pallas_call(functools.partial(halo_kernel, nx, ny, rows, cols), out_sh...  14.5 us
    pallas_call x1, Pallas kernels, body(): pl.pallas_call(functools.partial(reduce_kernel, nx, ny, float(rows * cols...  13.9 us
    unnamed x22, local copies, waits for them, and re-layouts  7.13 us

commit v1 on v0

v1 whole, which is shorter than its diff:
```python
import functools
import math

import jax
import jax.numpy as jnp
import numpy as np
from jax import lax
from jax.experimental import pallas as pl
from jax.experimental.pallas import tpu as pltpu
from jax.sharding import PartitionSpec as P

NZ = 32
H = 32
KC = 64
S = 256
LANES = 128
TILES = NZ * KC // LANES
CHUNK = 4
PIECES = 4

base_freq = 0.1
norm_eps = 1e-06
MESH = pl.DeviceIdType.MESH


def tables():
    orders = np.arange(1, H + 1, dtype=np.float64)
    angles = orders[:, None] * (2.0 * math.pi * np.arange(S) / S)[None, :]
    synthesis = np.concatenate([np.cos(angles), np.sin(angles)], axis=0)
    analysis = synthesis.T * (2.0 / S)
    derived = np.concatenate(
        [base_freq * orders * analysis[:, H:], -base_freq * orders * analysis[:, :H]], axis=1
    )

    def pair(table):
        zeros = np.zeros_like(table)
        return np.block([[table, zeros], [zeros, table]])

    def split(table):
        high = table.astype(jnp.bfloat16)
        low = (table - high.astype(np.float64)).astype(jnp.bfloat16)
        return high, low

    high, _ = split(pair(synthesis))
    forward = np.concatenate([high, high], axis=0)
    high, low = split(0.5 * np.concatenate([pair(analysis), pair(derived)], axis=0))
    return jnp.asarray(forward), jnp.asarray(np.concatenate([high, low], axis=1))


def lookup(region, table, count):
    value = jnp.where(region == 0, table[0], 0.0)
    for r in range(1, count):
        value = jnp.where(region == r, table[r], value)
    return value


def harmonic_mean(left, right):
    return 2.0 * left * right / (left + right)


def spread(cells, tile, lane, base=0):
    index = base + 2 * tile + (lane >= KC).astype(jnp.int32)
    return jnp.take_along_axis(cells, index, axis=1, mode="promise_in_bounds")


def square_sum(value):
    return jnp.sum((value * value).reshape(-1, 8, LANES), axis=0)


def kernel(
    nx, ny, rows, cols, regions,
    volt_hbm, drive_hbm, region_hbm, mask_hbm, sigma_hbm, cap_hbm, forward_hbm, back_hbm,
    out_ref, norm_ref,
    volt_buf, drive_buf, region_buf, mask_buf, end_region, side_buf, side_region,
    sigma_ref, cap_ref, forward_ref, back_ref, cell_buf, turn_buf, flux_buf, acc_ref, got,
    volt_sem, drive_sem, misc_sem, row_send, row_recv, side_send, side_recv, norm_send, norm_recv,
):
    me_x, me_y = lax.axis_index("gx"), lax.axis_index("gy")
    up, down = lax.rem(me_x + 1, nx), lax.rem(me_x + nx - 1, nx)
    has_left, has_right = me_y > 0, me_y < ny - 1
    barrier = pltpu.get_barrier_semaphore()

    for dx in range(nx):
        for dy in range(ny):
            if dx or dy:
                peer = (lax.rem(me_x + dx, nx), lax.rem(me_y + dy, ny))
                pl.semaphore_signal(barrier, inc=1, device_id=peer, device_id_type=MESH)

    def volt_copy(row):
        return pltpu.make_async_copy(volt_hbm.at[row], volt_buf.at[row + 1], volt_sem.at[row])

    def drive_copy(row):
        return pltpu.make_async_copy(drive_hbm.at[row], drive_buf.at[row], drive_sem.at[row])

    misc = [
        pltpu.make_async_copy(region_hbm, region_buf, misc_sem.at[0]),
        pltpu.make_async_copy(mask_hbm, mask_buf, misc_sem.at[1]),
        pltpu.make_async_copy(sigma_hbm, sigma_ref, misc_sem.at[2]),
        pltpu.make_async_copy(cap_hbm, cap_ref, misc_sem.at[3]),
        pltpu.make_async_copy(forward_hbm, forward_ref, misc_sem.at[4]),
        pltpu.make_async_copy(back_hbm, back_ref, misc_sem.at[5]),
    ]
    volt_copy(rows - 1).start()
    volt_copy(0).start()
    for c in misc:
        c.start()
    for row in range(rows):
        if 0 < row < rows - 1:
            volt_copy(row).start()
        drive_copy(row).start()

    def remote(source, target, send, recv, axis, peer):
        return pltpu.make_async_remote_copy(
            src_ref=source, dst_ref=target, send_sem=send, recv_sem=recv,
            device_id={axis: peer}, device_id_type=MESH,
        )

    row_copies = [
        remote(region_buf.at[rows - 1], end_region.at[0], row_send.at[0], row_recv.at[0], "gx", up),
        remote(region_buf.at[0], end_region.at[1], row_send.at[1], row_recv.at[1], "gx", down),
    ]
    piece = TILES // PIECES * LANES
    for p in range(PIECES):
        lanes = pl.ds(p * piece, piece)
        for k, (source, target, peer) in enumerate(((rows, 0, up), (1, rows + 1, down))):
            n = 2 + 2 * p + k
            row_copies.append(remote(
                volt_buf.at[source, :, lanes], volt_buf.at[target, :, lanes],
                row_send.at[n], row_recv.at[n], "gx", peer,
            ))
    to_right = [
        remote(volt_hbm.at[:, pl.ds(cols - 1, 1), :], side_buf.at[0], side_send.at[0],
               side_recv.at[0], "gy", me_y + 1),
        remote(region_buf, side_region.at[0], side_send.at[1], side_recv.at[1], "gy", me_y + 1),
    ]
    to_left = [
        remote(volt_hbm.at[:, pl.ds(0, 1), :], side_buf.at[1], side_send.at[2],
               side_recv.at[2], "gy", me_y - 1),
        remote(region_buf, side_region.at[1], side_send.at[3], side_recv.at[3], "gy", me_y - 1),
    ]

    volt_copy(rows - 1).wait()
    volt_copy(0).wait()
    misc[0].wait()
    pl.semaphore_wait(barrier, nx * ny - 1)
    for c in row_copies:
        c.start()

    @pl.when(has_right)
    def _():
        for c in to_right:
            c.start()

    @pl.when(has_left)
    def _():
        for c in to_left:
            c.start()

    for c in misc[1:4]:
        c.wait()
    turn_buf[...] = jnp.zeros_like(turn_buf)

    for i in range(rows):
        turn_buf[i, :NZ, :cols] = lookup(region_buf[i], sigma_ref, regions)
        turn_buf[i, NZ : 2 * NZ, :cols] = lookup(region_buf[i], cap_ref, regions)
        turn_buf[i, 2 * NZ : 3 * NZ, :cols] = mask_buf[i].astype(jnp.float32)
    for i in range(rows):
        cell_buf[i] = turn_buf[i].T[:cols]
    flux_buf[...] = jnp.zeros_like(flux_buf)
    acc_ref[...] = jnp.zeros_like(acc_ref)
    misc[4].wait()
    misc[5].wait()

    lane = lax.broadcasted_iota(jnp.int32, (cols, LANES), 1)
    col = lax.broadcasted_iota(jnp.int32, (cols, LANES), 0)
    first = lane < KC
    half = lane % KC
    order = base_freq * (half % H + 1).astype(jnp.float32)
    order = jnp.where(half < H, order, -order)
    swap = lane ^ H

    def row_step(i, _):
        @pl.when(i < rows - 2)
        def _():
            volt_copy(i + 1).wait()

        drive_copy(i).wait()
        cells = cell_buf[i]
        after = jnp.minimum(i + 1, rows - 1)
        g_high = harmonic_mean(cells, cell_buf[after])
        g_col = harmonic_mean(cells, pltpu.roll(cells, cols - 1, 0))
        g_col = jnp.where(col == cols - 1, 0.0, g_col)
        g_depth = harmonic_mean(cells, pltpu.roll(cells, LANES - 1, 1))
        g_depth = jnp.where(lane < NZ - 1, g_depth, 0.0)
        prev_flux = None
        total = jnp.zeros((8, LANES), jnp.float32)
        for start in range(0, TILES, CHUNK):
            xs = []
            for t in range(start, start + CHUNK):
                v = volt_buf[i + 1, :, t * LANES : (t + 1) * LANES]
                high = v.astype(jnp.bfloat16)
                low = (v - high.astype(jnp.float32)).astype(jnp.bfloat16)
                xs.append(jnp.concatenate([high, low], axis=1))
            samples = jnp.dot(
                jnp.concatenate(xs, axis=0), forward_ref[...], preferred_element_type=jnp.float32
            )
            size = jnp.abs(samples)
            small = jnp.exp2(size * (-2.0 / math.log(2.0)) - 1.0)
            even = (size + jnp.log(0.5 + small)).astype(jnp.bfloat16)
            charge = jnp.tanh(samples.astype(jnp.bfloat16))
            projected = jnp.dot(
                jnp.concatenate([even, charge], axis=1), back_ref[...],
                preferred_element_type=jnp.float32,
            )
            projected = projected[:, :LANES] + projected[:, LANES:]
            for t in range(start, start + CHUNK):
                at = slice(t * LANES, (t + 1) * LANES)
                v = volt_buf[i + 1, :, at]
                flux = spread(g_high, t, lane) * (volt_buf[after + 1, :, at] - v)
                value = flux_buf[:, at] - flux
                flux_buf[:, at] = flux
                flux = spread(g_col, t, lane) * (pltpu.roll(v, cols - 1, 0) - v)
                value += pltpu.roll(flux, 1, 0) - flux
                ahead = volt_buf[i + 1, :, (t + 1) * LANES : (t + 2) * LANES] if t + 1 < TILES else v
                deep = pltpu.roll(jnp.where(first, ahead, v), KC, 1)
                flux = spread(g_depth, t, lane) * (deep - v)
                flux_r = pltpu.roll(flux, KC, 1)
                before = jnp.zeros_like(flux_r) if prev_flux is None else prev_flux
                value += jnp.where(first, before, flux_r) - flux
                prev_flux = flux_r
                swapped = jnp.take_along_axis(v, swap, axis=1, mode="promise_in_bounds")
                value += spread(cells, t, lane, NZ) * (order * swapped)
                rows_of = slice((t - start) * cols, (t - start + 1) * cols)
                value += spread(cells, t, lane, 2 * NZ) * (projected[rows_of] + 0.5 * v)
                value -= drive_buf[i, :, at]
                out_ref[i, :, at] = value
                total += square_sum(value[8 : cols - 8])
        inside = jnp.logical_and(i > 0, i < rows - 1)
        acc_ref[...] += jnp.where(inside, total, 0.0)
        return 0

    lax.fori_loop(0, rows, row_step, 0)

    lane8, sub8 = lane[:8], col[:8]

    def side_step(side):
        edge = 0 if side == 0 else cols - 8
        line = 0 if side == 0 else 7
        there = cols - 1 if side == 0 else 0

        def step(i, _):
            turn_buf[i, :NZ, :cols] = lookup(side_region[side, i], sigma_ref, regions)
            near = jnp.broadcast_to(turn_buf[i].T[there : there + 1], (8, LANES))
            g = harmonic_mean(cell_buf[i, edge : edge + 8], near)
            g = jnp.where(sub8 == line, g, 0.0)
            for t in range(TILES):
                at = slice(t * LANES, (t + 1) * LANES)
                v = volt_buf[i + 1, edge : edge + 8, at]
                far = jnp.broadcast_to(side_buf[side, i, :, at], (8, LANES))
                out_ref[i, edge : edge + 8, at] += spread(g, t, lane8) * (v - far)
            return 0

        return step

    @pl.when(has_left)
    def _():
        for c in to_right:
            c.wait_recv()
        lax.fori_loop(0, rows, side_step(0), 0)

    @pl.when(has_right)
    def _():
        for c in to_left:
            c.wait_recv()
        lax.fori_loop(0, rows, side_step(1), 0)

    def edge_squares(i, total):
        for t in range(TILES):
            at = slice(t * LANES, (t + 1) * LANES)
            total += square_sum(out_ref[i, :8, at]) + square_sum(out_ref[i, cols - 8 :, at])
        return total

    total = lax.fori_loop(1, rows - 1, edge_squares, acc_ref[...])

    row_copies[0].wait_recv()
    row_copies[1].wait_recv()
    ends = []
    for k in range(2):
        turn_buf[k, :NZ, :cols] = lookup(end_region[k], sigma_ref, regions)
    for k, i in ((0, 0), (1, rows - 1)):
        ends.append(harmonic_mean(cell_buf[i], turn_buf[k].T[:cols]))
    for p in range(PIECES):
        for k, i in ((0, 0), (1, rows - 1)):
            row_copies[2 + 2 * p + k].wait_recv()
            for t in range(p * TILES // PIECES, (p + 1) * TILES // PIECES):
                at = slice(t * LANES, (t + 1) * LANES)
                v = volt_buf[i + 1, :, at]
                value = out_ref[i, :, at]
                value += spread(ends[k], t, lane) * (v - volt_buf[k * (rows + 1), :, at])
                out_ref[i, :, at] = value
                total += square_sum(value)

    here = me_x * ny + me_y
    got[here] = jnp.sum(total, axis=0, keepdims=True)

    for c in row_copies:
        c.wait_send()

    @pl.when(has_right)
    def _():
        for c in to_right:
            c.wait_send()

    @pl.when(has_left)
    def _():
        for c in to_left:
            c.wait_send()

    def norm_copy(dx, dy, sent):
        x, y = lax.rem(me_x + dx, nx), lax.rem(me_y + dy, ny)
        slot = here if sent else x * ny + y
        return pltpu.make_async_remote_copy(
            src_ref=got.at[here], dst_ref=got.at[slot],
            send_sem=norm_send.at[x * ny + y], recv_sem=norm_recv.at[slot],
            device_id=(x, y), device_id_type=MESH,
        )

    peers = [(dx, dy) for dx in range(nx) for dy in range(ny) if dx or dy]
    for dx, dy in peers:
        norm_copy(dx, dy, True).start()
    for dx, dy in peers:
        norm_copy(dx, dy, False).wait_recv()
    value = jnp.broadcast_to(jnp.sum(got[...], axis=0), (8, LANES))
    value = value + pltpu.roll(value, KC, 1)
    value = jnp.sqrt(value / float(rows * cols * NZ * nx * ny) + norm_eps)
    norm_ref[...] = value[:1, :KC]
    for dx, dy in peers:
        norm_copy(dx, dy, True).wait_send()


def write_kernel(residual, norms, residual_out, norms_out, sems):
    copies = [
        pltpu.make_async_copy(residual, residual_out, sems.at[0]),
        pltpu.make_async_copy(norms, norms_out, sems.at[1]),
    ]
    for c in copies:
        c.start()
    for c in copies:
        c.wait()


def body(volt, drive, region, diode_mask, sigma_table, cap_table):
    rows, cols, width = volt.shape
    regions = sigma_table.shape[0]
    nx, ny = lax.axis_size("gx"), lax.axis_size("gy")
    n = nx * ny
    region = jnp.transpose(region, (0, 2, 1))
    diode_mask = jnp.transpose(diode_mask, (0, 2, 1))
    forward, back = tables()
    hbm = pl.BlockSpec(memory_space=pltpu.HBM)
    vmem = pl.BlockSpec(memory_space=pltpu.VMEM)
    dma = pltpu.SemaphoreType.DMA
    residual, norms = pl.pallas_call(
        functools.partial(kernel, nx, ny, rows, cols, regions),
        out_shape=(
            pltpu.VMEM(volt.shape, jnp.float32),
            pltpu.VMEM((1, KC), jnp.float32),
        ),
        in_specs=[hbm] * 8,
        out_specs=(vmem, vmem),
        scratch_shapes=[
            pltpu.VMEM((rows + 2, cols, width), jnp.float32),
            pltpu.VMEM((rows, cols, width), jnp.float32),
            pltpu.VMEM((rows, NZ, cols), jnp.int32),
            pltpu.VMEM((rows, NZ, cols), jnp.int32),
            pltpu.VMEM((2, NZ, cols), jnp.int32),
            pltpu.VMEM((2, rows, 1, width), jnp.float32),
            pltpu.VMEM((2, rows, NZ, cols), jnp.int32),
            pltpu.SMEM((regions,), jnp.float32),
            pltpu.SMEM((regions,), jnp.float32),
            pltpu.VMEM(forward.shape, jnp.bfloat16),
            pltpu.VMEM(back.shape, jnp.bfloat16),
            pltpu.VMEM((rows, cols, LANES), jnp.float32),
            pltpu.VMEM((rows, LANES, LANES), jnp.float32),
            pltpu.VMEM((cols, width), jnp.float32),
            pltpu.VMEM((8, LANES), jnp.float32),
            pltpu.VMEM((n, 1, LANES), jnp.float32),
            dma((rows,)),
            dma((rows,)),
            dma((6,)),
            dma((2 + 2 * PIECES,)),
            dma((2 + 2 * PIECES,)),
            dma((4,)),
            dma((4,)),
            dma((n,)),
            dma((n,)),
        ],
        compiler_params=pltpu.CompilerParams(
            collective_id=0, has_side_effects=True, vmem_limit_bytes=50 * 2**20
        ),
        name="balance",
    )(volt, drive, region, diode_mask, sigma_table, cap_table, forward, back)
    residual, norms = pl.pallas_call(
        write_kernel,
        out_shape=(
            jax.ShapeDtypeStruct(volt.shape, jnp.float32),
            jax.ShapeDtypeStruct((1, KC), jnp.float32),
        ),
        in_specs=[vmem, vmem],
        out_specs=(hbm, hbm),
        scratch_shapes=[dma((2,))],
        compiler_params=pltpu.CompilerParams(vmem_limit_bytes=2**20),
        name="write",
    )(residual, norms)
    return residual, norms.reshape(KC)


def solution(mesh):
    return jax.shard_map(
        body,
        mesh=mesh,
        in_specs=(
            P("gx", "gy", None),
            P("gx", "gy", None),
            P("gx", "gy", None),
            P("gx", "gy", None),
            P(),
            P(),
        ),
        out_specs=(P("gx", "gy", None), P()),
        check_vma=False,
    )
```

time: 65.4 us -> 39.1 us (0.60)
  Pallas kernels: 56 us -> 38.3 us
  local copies, waits for them, and re-layouts: 8.32 us -> 0 us
    pallas_call x3 -> x2, Pallas kernels: 56 us -> 38.3 us  [the longest x1 36.3 us: body(): pl.pallas_call(functools.partial(kernel, nx, ny, rows, cols, regions), ou...]
    unnamed x22 -> x0, local copies, waits for them, and re-layouts: 7.13 us -> none
    squeeze x1 -> x0, local copies, waits for them, and re-layouts: 1.18 us -> none  [body(): return (residual, norms[0, :KC])]
where the time goes in v1:
time: 39.1 us; the launch traced here: 39 us
  Pallas kernels  38.3 us (98%)
  between operations  0.64 us (2%)
    pallas_call x1, Pallas kernels, body(): pl.pallas_call(functools.partial(kernel, nx, ny, rows, cols, regions), ou...  36.3 us
    pallas_call x1, Pallas kernels, body(): pl.pallas_call(write_kernel, out_shape=(jax.ShapeDtypeStruct(volt.shape,...  2.03 us

profile of v1, /device:TPU:0, one launch (start us, length us, event | category | flops | bytes accessed | tf_op | source)
XLA Modules:
  0.0 39.0 jit_solution(11827181065311824448)
XLA Ops:
  0.6 36.3 %balance.1 = (f32[8,64,2048]{2,1,0:T(8,128)S(1)}, f32[1,64]{1,0:T(1,128)S(1)}) custom-call(f32[8,64,2048]{2,1,0:T(8,128)} %volt_hbm.1, f32[8,64,2048]{2,1,0:T(8,128)} %drive_hbm.1, s32[8,32,64]{2,1,0:T(8,128)} %bitcast.3, s32[8,32,64]{2,1,0:T(8,128)} %bitcast.4, f32[8]{0:T(128)} %sigma_hbm.1, f32[8]{0:T(128)} %cap_hbm.1, ...), custom_call_target="tpu_custom_call" | custom-call | tf_op jit(solution)/shard_map/balance/pallas_call | solution.py:363
  36.9 2.0 %write.1 = (f32[8,64,2048]{2,1,0:T(8,128)}, f32[1,64]{1,0:T(1,128)}) custom-call(f32[8,64,2048]{2,1,0:T(8,128)S(1)} %get-tuple-element.6.residual, f32[1,64]{1,0:T(1,128)S(1)} %get-tuple-element.7.norms), custom_call_target="tpu_custom_call" | custom-call | tf_op jit(solution)/shard_map/write/pallas_call | solution.py:403

commit v2 on v1

--- a/solution.py
+++ b/solution.py
@@ -15,8 +15,9 @@
 S = 256
 LANES = 128
 TILES = NZ * KC // LANES
-CHUNK = 4
-PIECES = 4
+CHUNK = 8
+PIECES = 2
+SEND = 0
 
 base_freq = 0.1
 norm_eps = 1e-06
@@ -44,7 +45,14 @@
     high, _ = split(pair(synthesis))
     forward = np.concatenate([high, high], axis=0)
     high, low = split(0.5 * np.concatenate([pair(analysis), pair(derived)], axis=0))
-    return jnp.asarray(forward), jnp.asarray(np.concatenate([high, low], axis=1))
+    back = np.concatenate([high, low], axis=1)
+    wide = CHUNK * LANES
+    place = np.zeros((4, NZ, TILES // CHUNK, 2, wide), jnp.bfloat16)
+    for z in range(NZ):
+        chunk, at = divmod(z * KC, wide)
+        for k in range(4):
+            place[k, z, chunk, k // 2, at : at + KC] = 1
+    return jnp.asarray(forward), jnp.asarray(back), jnp.asarray(place.reshape(4 * NZ, -1))
 
 
 def lookup(region, table, count):
@@ -58,21 +66,25 @@
     return 2.0 * left * right / (left + right)
 
 
-def spread(cells, tile, lane, base=0):
-    index = base + 2 * tile + (lane >= KC).astype(jnp.int32)
-    return jnp.take_along_axis(cells, index, axis=1, mode="promise_in_bounds")
-
-
-def square_sum(value):
-    return jnp.sum((value * value).reshape(-1, 8, LANES), axis=0)
+def packed(a, b):
+    parts = []
+    for g in (a, b):
+        high = g.astype(jnp.bfloat16).astype(jnp.float32)
+        parts += [high, g - high]
+    return jnp.concatenate(parts, axis=0).T.astype(jnp.bfloat16)
+
+
+def fold(value):
+    return jnp.sum(value.reshape(-1, 8, LANES), axis=0)
 
 
 def kernel(
     nx, ny, rows, cols, regions,
-    volt_hbm, drive_hbm, region_hbm, mask_hbm, sigma_hbm, cap_hbm, forward_hbm, back_hbm,
+    volt_hbm, drive_hbm, region_hbm, mask_hbm, sigma_hbm, cap_hbm, forward_hbm, back_hbm, place_hbm,
     out_ref, norm_ref,
     volt_buf, drive_buf, region_buf, mask_buf, end_region, side_buf, side_region,
-    sigma_ref, cap_ref, forward_ref, back_ref, cell_buf, turn_buf, flux_buf, acc_ref, got,
+    sigma_ref, cap_ref, forward_ref, back_ref, place_ref, cond_buf, edge_buf, flux_buf, line_buf,
+    acc_ref, got,
     volt_sem, drive_sem, misc_sem, row_send, row_recv, side_send, side_recv, norm_send, norm_recv,
 ):
     me_x, me_y = lax.axis_index("gx"), lax.axis_index("gy")
@@ -99,14 +111,17 @@
         pltpu.make_async_copy(cap_hbm, cap_ref, misc_sem.at[3]),
         pltpu.make_async_copy(forward_hbm, forward_ref, misc_sem.at[4]),
         pltpu.make_async_copy(back_hbm, back_ref, misc_sem.at[5]),
+        pltpu.make_async_copy(place_hbm, place_ref, misc_sem.at[6]),
     ]
-    volt_copy(rows - 1).start()
     volt_copy(0).start()
+    volt_copy(1).start()
     for c in misc:
         c.start()
-    for row in range(rows):
-        if 0 < row < rows - 1:
-            volt_copy(row).start()
+    drive_copy(0).start()
+    volt_copy(rows - 1).start()
+    for row in range(2, rows - 1):
+        volt_copy(row).start()
+    for row in range(1, rows):
         drive_copy(row).start()
 
     def remote(source, target, send, recv, axis, peer):
@@ -129,70 +144,80 @@
                 row_send.at[n], row_recv.at[n], "gx", peer,
             ))
     to_right = [
-        remote(volt_hbm.at[:, pl.ds(cols - 1, 1), :], side_buf.at[0], side_send.at[0],
+        remote(volt_buf.at[pl.ds(1, rows), pl.ds(cols - 1, 1), :], side_buf.at[0], side_send.at[0],
                side_recv.at[0], "gy", me_y + 1),
         remote(region_buf, side_region.at[0], side_send.at[1], side_recv.at[1], "gy", me_y + 1),
     ]
     to_left = [
-        remote(volt_hbm.at[:, pl.ds(0, 1), :], side_buf.at[1], side_send.at[2],
+        remote(volt_buf.at[pl.ds(1, rows), pl.ds(0, 1), :], side_buf.at[1], side_send.at[2],
                side_recv.at[2], "gy", me_y - 1),
         remote(region_buf, side_region.at[1], side_send.at[3], side_recv.at[3], "gy", me_y - 1),
     ]
 
-    volt_copy(rows - 1).wait()
+    def send():
+        for row in range(2, rows):
+            volt_copy(row).wait()
+        pl.semaphore_wait(barrier, nx * ny - 1)
+        for c in row_copies:
+            c.start()
+
+        @pl.when(has_right)
+        def _():
+            for c in to_right:
+                c.start()
+
+        @pl.when(has_left)
+        def _():
+            for c in to_left:
+                c.start()
+
     volt_copy(0).wait()
-    misc[0].wait()
-    pl.semaphore_wait(barrier, nx * ny - 1)
-    for c in row_copies:
-        c.start()
-
-    @pl.when(has_right)
-    def _():
-        for c in to_right:
-            c.start()
-
-    @pl.when(has_left)
-    def _():
-        for c in to_left:
-            c.start()
-
-    for c in misc[1:4]:
+    volt_copy(1).wait()
+    for c in misc[:4]:
         c.wait()
-    turn_buf[...] = jnp.zeros_like(turn_buf)
-
-    for i in range(rows):
-        turn_buf[i, :NZ, :cols] = lookup(region_buf[i], sigma_ref, regions)
-        turn_buf[i, NZ : 2 * NZ, :cols] = lookup(region_buf[i], cap_ref, regions)
-        turn_buf[i, 2 * NZ : 3 * NZ, :cols] = mask_buf[i].astype(jnp.float32)
-    for i in range(rows):
-        cell_buf[i] = turn_buf[i].T[:cols]
-    flux_buf[...] = jnp.zeros_like(flux_buf)
-    acc_ref[...] = jnp.zeros_like(acc_ref)
-    misc[4].wait()
-    misc[5].wait()
-
     lane = lax.broadcasted_iota(jnp.int32, (cols, LANES), 1)
-    col = lax.broadcasted_iota(jnp.int32, (cols, LANES), 0)
     first = lane < KC
     half = lane % KC
     order = base_freq * (half % H + 1).astype(jnp.float32)
     order = jnp.where(half < H, order, -order)
     swap = lane ^ H
+    lane_t = lane[:NZ]
+    depth_t = lax.broadcasted_iota(jnp.int32, (NZ, LANES), 0)
+
+    def padded(table):
+        rest = jnp.ones((NZ, LANES - cols), jnp.float32)
+        return jnp.concatenate([table, rest], axis=1)
+
+    for i in range(rows):
+        cond_buf[i] = padded(lookup(region_buf[i], sigma_ref, regions))
+    for i in range(rows):
+        cond = cond_buf[i]
+        g_high = harmonic_mean(cond, cond_buf[min(i + 1, rows - 1)])
+        g_col = harmonic_mean(cond, pltpu.roll(cond, LANES - 1, 1))
+        g_col = jnp.where(lane_t == cols - 1, 0.0, g_col)
+        g_deep = harmonic_mean(cond, pltpu.roll(cond, NZ - 1, 0))
+        g_deep = jnp.where(depth_t < NZ - 1, g_deep, 0.0)
+        cap = padded(lookup(region_buf[i], cap_ref, regions))
+        diode = padded(mask_buf[i].astype(jnp.float32))
+        edge_buf[i, 0] = packed(g_high, g_col)[:cols]
+        edge_buf[i, 1] = packed(g_deep, cap)[:cols]
+        edge_buf[i, 2] = packed(diode, diode)[:cols]
+    flux_buf[...] = jnp.zeros_like(flux_buf)
+    acc_ref[...] = jnp.zeros_like(acc_ref)
+    for c in misc[4:]:
+        c.wait()
+    wide = CHUNK * LANES
+
+    def placed(edges, start, count=2):
+        at = start * LANES * 2
+        table = place_ref[:, at : at + count * wide]
+        return jnp.dot(edges, table, preferred_element_type=jnp.float32)
 
     def row_step(i, _):
-        @pl.when(i < rows - 2)
-        def _():
-            volt_copy(i + 1).wait()
-
+        pl.when(i == SEND)(send)
         drive_copy(i).wait()
-        cells = cell_buf[i]
-        after = jnp.minimum(i + 1, rows - 1)
-        g_high = harmonic_mean(cells, cell_buf[after])
-        g_col = harmonic_mean(cells, pltpu.roll(cells, cols - 1, 0))
-        g_col = jnp.where(col == cols - 1, 0.0, g_col)
-        g_depth = harmonic_mean(cells, pltpu.roll(cells, LANES - 1, 1))
-        g_depth = jnp.where(lane < NZ - 1, g_depth, 0.0)
-        prev_flux = None
+        after = jnp.minimum(i + 2, rows)
+        before = None
         total = jnp.zeros((8, LANES), jnp.float32)
         for start in range(0, TILES, CHUNK):
             xs = []
@@ -213,92 +238,90 @@
                 preferred_element_type=jnp.float32,
             )
             projected = projected[:, :LANES] + projected[:, LANES:]
+            pairs = placed(edge_buf[i, :2].reshape(2 * cols, LANES), start)
+            diodes = placed(edge_buf[i, 2], start, 1)
             for t in range(start, start + CHUNK):
                 at = slice(t * LANES, (t + 1) * LANES)
+                one = slice((t - start) * LANES, (t - start + 1) * LANES)
+                two = slice(wide + (t - start) * LANES, wide + (t - start + 1) * LANES)
                 v = volt_buf[i + 1, :, at]
-                flux = spread(g_high, t, lane) * (volt_buf[after + 1, :, at] - v)
+                flux = pairs[:cols, one] * (volt_buf[after, :, at] - v)
                 value = flux_buf[:, at] - flux
                 flux_buf[:, at] = flux
-                flux = spread(g_col, t, lane) * (pltpu.roll(v, cols - 1, 0) - v)
+                flux = pairs[:cols, two] * (pltpu.roll(v, cols - 1, 0) - v)
                 value += pltpu.roll(flux, 1, 0) - flux
                 ahead = volt_buf[i + 1, :, (t + 1) * LANES : (t + 2) * LANES] if t + 1 < TILES else v
                 deep = pltpu.roll(jnp.where(first, ahead, v), KC, 1)
-                flux = spread(g_depth, t, lane) * (deep - v)
+                flux = pairs[cols:, one] * (deep - v)
                 flux_r = pltpu.roll(flux, KC, 1)
-                before = jnp.zeros_like(flux_r) if prev_flux is None else prev_flux
-                value += jnp.where(first, before, flux_r) - flux
-                prev_flux = flux_r
+                value += jnp.where(first, jnp.zeros_like(flux_r) if before is None else before, flux_r)
+                value -= flux
+                before = flux_r
                 swapped = jnp.take_along_axis(v, swap, axis=1, mode="promise_in_bounds")
-                value += spread(cells, t, lane, NZ) * (order * swapped)
+                value += pairs[cols:, two] * (order * swapped)
                 rows_of = slice((t - start) * cols, (t - start + 1) * cols)
-                value += spread(cells, t, lane, 2 * NZ) * (projected[rows_of] + 0.5 * v)
+                value += diodes[:, one] * (projected[rows_of] + 0.5 * v)
                 value -= drive_buf[i, :, at]
                 out_ref[i, :, at] = value
-                total += square_sum(value[8 : cols - 8])
-        inside = jnp.logical_and(i > 0, i < rows - 1)
-        acc_ref[...] += jnp.where(inside, total, 0.0)
+                total += fold(value * value)
+        acc_ref[...] += total
         return 0
 
     lax.fori_loop(0, rows, row_step, 0)
 
-    lane8, sub8 = lane[:8], col[:8]
-
-    def side_step(side):
-        edge = 0 if side == 0 else cols - 8
-        line = 0 if side == 0 else 7
-        there = cols - 1 if side == 0 else 0
-
-        def step(i, _):
-            turn_buf[i, :NZ, :cols] = lookup(side_region[side, i], sigma_ref, regions)
-            near = jnp.broadcast_to(turn_buf[i].T[there : there + 1], (8, LANES))
-            g = harmonic_mean(cell_buf[i, edge : edge + 8], near)
-            g = jnp.where(sub8 == line, g, 0.0)
+    sub8 = lax.broadcasted_iota(jnp.int32, (8, LANES), 0)
+
+    def side(k, copies):
+        for c in copies:
+            c.wait_recv()
+        mine, theirs = (0, cols - 1) if k == 0 else (cols - 1, 0)
+        edge, line = mine // 8 * 8, mine % 8
+        g = jnp.zeros((NZ, LANES), jnp.float32)
+        for i in range(rows):
+            far = padded(lookup(side_region[k, i], sigma_ref, regions))
+            far = pltpu.roll(far, (i - theirs) % LANES, 1)
+            near = pltpu.roll(cond_buf[i], (i - mine) % LANES, 1)
+            g = jnp.where(lane_t == i, harmonic_mean(near, far), g)
+        edges = packed(g, g)[:8]
+        for start in range(0, TILES, CHUNK):
+            line_buf[:, start * LANES : (start + CHUNK) * LANES] = placed(edges, start, 1)
+        total = jnp.zeros((8, LANES), jnp.float32)
+        for i in range(rows):
             for t in range(TILES):
                 at = slice(t * LANES, (t + 1) * LANES)
-                v = volt_buf[i + 1, edge : edge + 8, at]
-                far = jnp.broadcast_to(side_buf[side, i, :, at], (8, LANES))
-                out_ref[i, edge : edge + 8, at] += spread(g, t, lane8) * (v - far)
-            return 0
-
-        return step
-
-    @pl.when(has_left)
-    def _():
-        for c in to_right:
-            c.wait_recv()
-        lax.fori_loop(0, rows, side_step(0), 0)
-
-    @pl.when(has_right)
-    def _():
-        for c in to_left:
-            c.wait_recv()
-        lax.fori_loop(0, rows, side_step(1), 0)
-
-    def edge_squares(i, total):
-        for t in range(TILES):
-            at = slice(t * LANES, (t + 1) * LANES)
-            total += square_sum(out_ref[i, :8, at]) + square_sum(out_ref[i, cols - 8 :, at])
-        return total
-
-    total = lax.fori_loop(1, rows - 1, edge_squares, acc_ref[...])
+                far = jnp.broadcast_to(side_buf[k, i, :, at], (8, LANES))
+                g = jnp.broadcast_to(line_buf[i : i + 1, at], (8, LANES))
+                g = jnp.where(sub8 == line, g, 0.0)
+                change = g * (volt_buf[i + 1, edge : edge + 8, at] - far)
+                old = out_ref[i, edge : edge + 8, at]
+                out_ref[i, edge : edge + 8, at] = old + change
+                total += change * (2.0 * old + change)
+        acc_ref[...] += total
+
+    pl.when(has_left)(lambda: side(0, to_right))
+    pl.when(has_right)(lambda: side(1, to_left))
 
     row_copies[0].wait_recv()
     row_copies[1].wait_recv()
-    ends = []
-    for k in range(2):
-        turn_buf[k, :NZ, :cols] = lookup(end_region[k], sigma_ref, regions)
-    for k, i in ((0, 0), (1, rows - 1)):
-        ends.append(harmonic_mean(cell_buf[i], turn_buf[k].T[:cols]))
-    for p in range(PIECES):
+    g_low, g_high = (
+        harmonic_mean(cond_buf[i], padded(lookup(end_region[k], sigma_ref, regions)))
+        for k, i in ((0, 0), (1, rows - 1))
+    )
+    edges = packed(g_low, g_high)[:cols]
+    total = acc_ref[...]
+    for start in range(0, TILES, CHUNK):
+        if start % (TILES // PIECES) == 0:
+            for k in range(2):
+                row_copies[2 + 2 * (start * PIECES // TILES) + k].wait_recv()
+        ends = placed(edges, start)
         for k, i in ((0, 0), (1, rows - 1)):
-            row_copies[2 + 2 * p + k].wait_recv()
-            for t in range(p * TILES // PIECES, (p + 1) * TILES // PIECES):
+            for t in range(start, start + CHUNK):
                 at = slice(t * LANES, (t + 1) * LANES)
-                v = volt_buf[i + 1, :, at]
-                value = out_ref[i, :, at]
-                value += spread(ends[k], t, lane) * (v - volt_buf[k * (rows + 1), :, at])
-                out_ref[i, :, at] = value
-                total += square_sum(value)
+                one = slice(k * wide + (t - start) * LANES, k * wide + (t - start + 1) * LANES)
+                change = ends[:, one] * (volt_buf[i + 1, :, at] - volt_buf[k * (rows + 1), :, at])
+                old = out_ref[i, :, at]
+                out_ref[i, :, at] = old + change
+                total += fold(change * (2.0 * old + change))
 
     here = me_x * ny + me_y
     got[here] = jnp.sum(total, axis=0, keepdims=True)
@@ -356,7 +379,7 @@
     n = nx * ny
     region = jnp.transpose(region, (0, 2, 1))
     diode_mask = jnp.transpose(diode_mask, (0, 2, 1))
-    forward, back = tables()
+    forward, back, place = tables()
     hbm = pl.BlockSpec(memory_space=pltpu.HBM)
     vmem = pl.BlockSpec(memory_space=pltpu.VMEM)
     dma = pltpu.SemaphoreType.DMA
@@ -366,7 +389,7 @@
             pltpu.VMEM(volt.shape, jnp.float32),
             pltpu.VMEM((1, KC), jnp.float32),
         ),
-        in_specs=[hbm] * 8,
+        in_specs=[hbm] * 9,
         out_specs=(vmem, vmem),
         scratch_shapes=[
             pltpu.VMEM((rows + 2, cols, width), jnp.float32),
@@ -380,14 +403,16 @@
             pltpu.SMEM((regions,), jnp.float32),
             pltpu.VMEM(forward.shape, jnp.bfloat16),
             pltpu.VMEM(back.shape, jnp.bfloat16),
-            pltpu.VMEM((rows, cols, LANES), jnp.float32),
-            pltpu.VMEM((rows, LANES, LANES), jnp.float32),
+            pltpu.VMEM(place.shape, jnp.bfloat16),
+            pltpu.VMEM((rows, NZ, LANES), jnp.float32),
+            pltpu.VMEM((rows, 3, cols, LANES), jnp.bfloat16),
             pltpu.VMEM((cols, width), jnp.float32),
+            pltpu.VMEM((8, width), jnp.float32),
             pltpu.VMEM((8, LANES), jnp.float32),
             pltpu.VMEM((n, 1, LANES), jnp.float32),
             dma((rows,)),
             dma((rows,)),
-            dma((6,)),
+            dma((7,)),
             dma((2 + 2 * PIECES,)),
             dma((2 + 2 * PIECES,)),
             dma((4,)),
@@ -399,7 +424,7 @@
             collective_id=0, has_side_effects=True, vmem_limit_bytes=50 * 2**20
         ),
         name="balance",
-    )(volt, drive, region, diode_mask, sigma_table, cap_table, forward, back)
+    )(volt, drive, region, diode_mask, sigma_table, cap_table, forward, back, place)
     residual, norms = pl.pallas_call(
         write_kernel,
         out_shape=(

time: 39.1 us -> 33.1 us (0.85)
  Pallas kernels: 38.3 us -> 32.3 us
    pallas_call x1, Pallas kernels: 36.3 us -> 30.2 us  [body(): pl.pallas_call(functools.partial(kernel, nx, ny, rows, cols, regions), ou...]
where the time goes in v2:
time: 33.1 us; the launch traced here: 32.9 us
  Pallas kernels  32.3 us (98%)
  between operations  0.64 us (2%)
    pallas_call x1, Pallas kernels, body(): pl.pallas_call(functools.partial(kernel, nx, ny, rows, cols, regions), ou...  30.2 us
    pallas_call x1, Pallas kernels, body(): pl.pallas_call(write_kernel, out_shape=(jax.ShapeDtypeStruct(volt.shape,...  2.03 us

profile of v2, /device:TPU:0, one launch (start us, length us, event | category | flops | bytes accessed | tf_op | source)
XLA Modules:
  0.0 32.9 jit_solution(425515712761373013)
XLA Ops:
  0.6 30.2 %balance.1 = (f32[8,64,2048]{2,1,0:T(8,128)S(1)}, f32[1,64]{1,0:T(1,128)S(1)}) custom-call(f32[8,64,2048]{2,1,0:T(8,128)} %volt_hbm.1, f32[8,64,2048]{2,1,0:T(8,128)} %drive_hbm.1, s32[8,32,64]{2,1,0:T(8,128)} %bitcast.3, s32[8,32,64]{2,1,0:T(8,128)} %bitcast.4, f32[8]{0:T(128)} %sigma_hbm.1, f32[8]{0:T(128)} %cap_hbm.1, ...), custom_call_target="tpu_custom_call" | custom-call | tf_op jit(solution)/shard_map/balance/pallas_call | solution.py:386
  30.9 2.0 %write.1 = (f32[8,64,2048]{2,1,0:T(8,128)}, f32[1,64]{1,0:T(1,128)}) custom-call(f32[8,64,2048]{2,1,0:T(8,128)S(1)} %get-tuple-element.6.residual, f32[1,64]{1,0:T(1,128)S(1)} %get-tuple-element.7.norms), custom_call_target="tpu_custom_call" | custom-call | tf_op jit(solution)/shard_map/write/pallas_call | solution.py:428
